TPU v7x, 32 devices: a whole 2x2x4 slice. The times are simulated.
32 devices in a mesh: dp: 16 (over z, y, core), level: 2 (over x).
Axes of the slice: x: 2, y: 2, z: 4, core: 2. Of those that a mesh axis runs over, the one named last changes fastest.
Arguments:
- token_ids: int32 [16, 2, 1536], P('dp', 'level'), may hold values from 0 to 1023
- decoded_mask: int32 [16, 2, 1536], P('dp', 'level'), may hold values 0 or 1
- levels_done: int32 [16], P('dp'), may hold values from 0 to 1
- code_tables: bfloat16 [2, 1024, 1024], P('level'), may hold values from -6 to 6
- mask_vectors: bfloat16 [2, 1024], P('level'), may hold values from -6 to 6
- w_qkv: bfloat16 [3, 1024, 1024], P(None, 'dp', 'level'), may hold values from -6 to 6
- w_out: bfloat16 [1024, 1024], P('level', 'dp'), may hold values from -0.1875 to 0.1875
- w_expand: bfloat16 [1024, 2048], P('dp'), may hold values from -0.1875 to 0.1875
- w_depth: bfloat16 [5, 1024], replicated, may hold values from -2.5 to 2.5
- w_project: bfloat16 [1024, 1024], P('dp'), may hold values from -0.1875 to 0.1875
- level_heads: bfloat16 [2, 1024, 1024], P('level'), may hold values from -0.1875 to 0.1875
Outputs:
- logits: bfloat16 [16, 2, 1536, 1024], P('dp', 'level')
Inputs may be any that keep to these rules, and one draw needn't show every extreme that they name: `levels_done`: levels below it are fully decoded; the level equal to it is the one being decoded.
All inputs are finite; a program needn't handle non-finite values. No bound on the sum of `decoded_mask` on one device may be relied on, other than what follows from the above.
Results may differ from a plain program's by a relative error of at most 0.006.
Values may be sent and summed in bfloat16 or wider, within the bound.
A program may use at most 192 MiB of HBM per device.

v0:
```python
import jax
import jax.numpy as jnp
from jax import lax
from jax.sharding import PartitionSpec as P

HEADS = 16


def with_halo(x, sides, width):
    for axis, dim in sides:
        devices, length = (lax.axis_size(axis), x.shape[dim])
        up = [(i, (i + 1) % devices) for i in range(devices - 1)]
        down = [(j, i) for i, j in up]
        last = lax.slice_in_dim(x, length - width, length, axis=dim)
        leading = lax.slice_in_dim(x, 0, width, axis=dim)
        before = lax.ppermute(last, axis, up)
        after = lax.ppermute(leading, axis, down)
        x = jnp.concatenate([before, x, after], axis=dim)
    return x


def layer_norm(values):
    centered = values - jnp.mean(values, axis=-1, keepdims=True)
    variance = jnp.mean(centered * centered, axis=-1, keepdims=True)
    return centered * lax.rsqrt(variance + 1e-05)


def contract_with(left, shard_piece):
    return jnp.dot(left, shard_piece, preferred_element_type=jnp.float32)


def contract_three(left, shard_piece):
    return jnp.einsum("fk,jkc->jfc", left, shard_piece, preferred_element_type=jnp.float32)


def body(
    token_ids,
    decoded_mask,
    levels_done,
    code_tables,
    mask_vectors,
    w_qkv,
    w_out,
    w_expand,
    w_depth,
    w_project,
    level_heads,
):
    frames = token_ids.shape[2]
    model_width = code_tables.shape[2]
    groups = lax.axis_size("level")
    level_index = lax.axis_index("level")
    local_rows = frames // groups
    head_dim = model_width // HEADS
    scale = head_dim ** (-0.5)
    id_row = token_ids[0, 0]
    flag_row = decoded_mask[0, 0]
    done_count = levels_done[0]
    own_table = code_tables[0]
    fill_row = mask_vectors[0].astype(jnp.float32)
    all_live = level_index < done_count
    current = level_index == done_count
    use_token = all_live | current & (flag_row == 1)
    codes = lax.broadcasted_iota(jnp.int32, (frames, own_table.shape[0]), 1)
    onehot = (id_row[:, None] == codes).astype(jnp.bfloat16)
    picked = jnp.dot(onehot, own_table, preferred_element_type=jnp.float32)
    level_terms = (
        jnp.where(use_token[:, None], picked, fill_row[None, :])
        .astype(jnp.bfloat16)
        .reshape(groups, local_rows, model_width)
    )
    received = lax.all_to_all(level_terms, "level", split_axis=0, concat_axis=0, tiled=True)
    own_rows = jnp.sum(received, axis=0, dtype=jnp.float32)
    normed = layer_norm(own_rows).astype(jnp.bfloat16)
    full_columns = lax.all_gather(w_qkv, "level", axis=2, tiled=True)
    projected = contract_three(
        normed, lax.all_gather(full_columns, "dp", axis=1, tiled=True)
    ).astype(jnp.bfloat16)
    queries = projected[0].reshape(local_rows, HEADS, head_dim)
    running_max = jnp.full((HEADS, local_rows), -1e30, jnp.float32)
    accumulated = jnp.zeros((local_rows, HEADS, head_dim), jnp.float32)
    key_piece = lax.all_gather(projected[1], "level", axis=0, tiled=True)
    value_piece = lax.all_gather(projected[2], "level", axis=0, tiled=True)
    piece_rows = key_piece.shape[0]
    key_three = key_piece.reshape(piece_rows, HEADS, head_dim)
    value_three = value_piece.reshape(piece_rows, HEADS, head_dim)
    scores = (
        jnp.einsum("qhd,khd->hqk", queries, key_three, preferred_element_type=jnp.float32) * scale
    )
    new_max = jnp.maximum(running_max, jnp.max(scores, axis=-1))
    shrink = jnp.exp(running_max - new_max)
    weights = jnp.exp(scores - new_max[:, :, None])
    weight_sum = jnp.sum(weights, axis=-1)
    added = jnp.einsum(
        "hqk,khd->qhd",
        weights.astype(jnp.bfloat16),
        value_three,
        preferred_element_type=jnp.float32,
    )
    accumulated = accumulated * shrink.T[:, :, None] + added
    running_max, weight_sum, accumulated = (new_max, weight_sum, accumulated)
    attended = (
        (accumulated / weight_sum.T[:, :, None])
        .reshape(local_rows, model_width)
        .astype(jnp.bfloat16)
    )
    out_full = lax.all_gather(w_out, "level", axis=0, tiled=True)
    after_attn = own_rows + jnp.dot(
        attended,
        lax.all_gather(out_full, "dp", axis=1, tiled=True),
        preferred_element_type=jnp.float32,
    )
    normed_two = layer_norm(after_attn).astype(jnp.bfloat16)
    gate_linear = contract_with(normed_two, lax.all_gather(w_expand, "dp", axis=0, tiled=True))
    gated = (gate_linear[:, :model_width] * jax.nn.sigmoid(gate_linear[:, model_width:])).astype(
        jnp.bfloat16
    )
    half_width = w_depth.shape[0] // 2
    padded = with_halo(gated, (("level", 0),), half_width)
    conv = jnp.zeros((local_rows, model_width), jnp.float32)
    for tap_index in range(w_depth.shape[0]):
        conv = conv + padded[tap_index : tap_index + local_rows].astype(jnp.float32) * w_depth[
            tap_index
        ].astype(jnp.float32)
    activated = (conv * jax.nn.sigmoid(conv)).astype(jnp.bfloat16)
    after_conv = after_attn + contract_with(
        activated, lax.all_gather(w_project, "dp", axis=0, tiled=True)
    )
    final_norm = layer_norm(after_conv).astype(jnp.bfloat16)
    own_head = level_heads[0]
    logits = jnp.dot(
        lax.all_gather(final_norm, "level", axis=0, tiled=True),
        own_head,
        preferred_element_type=jnp.float32,
    ).astype(jnp.bfloat16)
    return logits[None, None]


def solution(mesh):
    return jax.shard_map(
        body,
        mesh=mesh,
        in_specs=(
            P("dp", "level", None),
            P("dp", "level", None),
            P("dp"),
            P("level", None, None),
            P("level", None),
            P(None, "dp", "level"),
            P("level", "dp"),
            P("dp", None),
            P(),
            P("dp", None),
            P("level", None, None),
        ),
        out_specs=P("dp", "level", None, None),
        check_vma=False,
    )
```

profile of v0, /device:TPU:0, one launch (start us, length us, event | category | flops | bytes accessed | tf_op | source)
XLA Modules:
  0.0 386.5 jit_solution(2967878390888933590)
XLA Ops:
  6.5 10.6 %all_gather.27 = bf16[3,64,1024]{2,1,0:T(8,128)(2,1)} all-gather(bf16[3,64,512]{2,1,0:T(8,128)(2,1)} %param.16), channel_id=1, replica_groups=mesh['dp'=16,'level'=2] {'level'}, dimensions={2}, use_global_device_ids=true | all-gather | bytes 589824 | tf_op jit(solution)/shard_map/all_gather | solution.py:75
  20.0 4.3 %select_convert_fusion = bf16[1536,1024]{1,0:T(8,128)(2,1)S(1)} fusion(f32[1024]{0:T(1024)S(1)} %bitcast.56, s32[1536]{0:T(1024)S(1)} %reduce.2, pred[1536]{0:T(1024)(128)(4,1)S(1)} %or_reduce_fusion, bf16[1,1024,1024]{2,1,0:T(8,128)(2,1)S(1)} %copy-done), kind=kOutput, calls=%fused_computation.7 | convolution fusion | flops 3224371200 | bytes 5254656 | tf_op jit(solution)/shard_map/dot_general | solution.py:66
  24.3 38.4 %all_to_all.5 = bf16[2,768,1024]{2,1,0:T(8,128)(2,1)S(1)} all-to-all(bf16[2,768,1024]{2,1,0:T(8,128)(2,1)S(1)} %bitcast.48), channel_id=1, replica_groups=mesh['dp'=16,'level'=2] {'level'}, dimensions={0} | all-to-all | bytes 6291456 | tf_op jit(solution)/shard_map/all_to_all | solution.py:72
  63.8 15.3 %all-gather.10.cloned.1.call-done = bf16[3,1024,1024]{2,1,0:T(8,128)(2,1)} async-done(((bf16[3,64,1024]{2,1,0:T(8,128)(2,1)}), bf16[3,1024,1024]{2,1,0:T(8,128)(2,1)}) %all-gather.10.cloned.1.call-update) | async-done | bytes 6291472 | tf_op jit(solution)/shard_map/all_gather | solution.py:77
  79.1 8.3 %convert_bitcast_fusion = bf16[3,768,1024]{2,1,0:T(8,128)(2,1)S(1)} fusion(bf16[3,1024,1024]{2,1,0:T(8,128)(2,1)} %all-gather.10.cloned.1.call-done, f32[768,1024]{1,0:T(8,128)S(1)} %get-tuple-element.6, f32[768]{0:T(1024)S(1)} %add_rsqrt_fusion.2, f32[768]{0:T(1024)S(1)} %broadcast_multiply_fusion.2), kind=kOutput, calls=%fused_computation.10 | convolution fusion | flops 4836556800 | bytes 14161920 | tf_op jit(solution)/shard_map/fk,jkc->jfc/dot_general | solution.py:33
  87.4 2.3 fusion.36
  90.5 5.0 %all_gather.31 = bf16[1024,64]{0,1:T(8,128)(2,1)} all-gather(bf16[512,64]{0,1:T(8,128)(2,1)S(1)} %copy-done.5), channel_id=1, replica_groups=mesh['dp'=16,'level'=2] {'level'}, dimensions={0}, use_global_device_ids=true | all-gather | bytes 196608 | tf_op jit(solution)/shard_map/all_gather | solution.py:107
  96.9 1.6 copy.15
  98.5 34.9 %all-gather.20.cloned.1.call-done = bf16[1,1536,1024]{2,1,0:T(8,128)(2,1)} async-done(((bf16[1,768,1024]{2,1,0:T(8,128)(2,1)}), bf16[1,1536,1024]{2,1,0:T(8,128)(2,1)}) %all-gather.20.cloned.1.call-update) | async-done | bytes 3145744 | tf_op jit(solution)/shard_map/all_gather | solution.py:82
  133.4 3.2 copy.16
  136.6 28.8 %multiply_reduce_fusion = (f32[16,768]{1,0:T(8,128)S(1)}, f32[16,768,1536]{2,1,0:T(8,128)}) fusion(bf16[768,16,64]{0,2,1:T(8,128)(2,1)} %bitcast.47, bf16[1536,16,64]{0,2,1:T(8,128)(2,1)S(1)} %bitcast.45), kind=kOutput, calls=%fused_computation.1 | convolution fusion | flops 2453655552 | bytes 80265216 | tf_op jit(solution)/shard_map/qhd,khd->hqk/dot_general | solution.py:88
  165.4 24.1 %fusion = f32[16,768]{1,0:T(8,128)S(1)} fusion(f32[16,768,1536]{2,1,0:T(8,128)} %get-tuple-element.20, f32[16,768]{1,0:T(8,128)S(1)} %get-tuple-element.13), kind=kLoop, calls=%fused_computation.2 | loop fusion | flops 56610816 | bytes 75595776 | tf_op jit(solution)/shard_map/reduce_sum | solution.py:93
  189.5 3.2 copy.17
  192.7 27.7 %fusion.11 = bf16[768,16,64]{0,2,1:T(8,128)(2,1)} fusion(bf16[1536,16,64]{0,2,1:T(8,128)(2,1)S(1)} %bitcast.46, f32[16,768,1536]{2,1,0:T(8,128)} %get-tuple-element.20, f32[16,768]{1,0:T(8,128)S(1)} %get-tuple-element.13, f32[768,16]{0,1:T(8,128)S(1)} %bitcast.50, f32[768,16]{0,1:T(8,128)S(1)} %get-tuple-element.12), kind=kOutput, calls=%fused_computation.20 | convolution fusion | flops 2474901504 | bytes 80363520 | tf_op jit(solution)/shard_map/hqk,khd->qhd/dot_general | solution.py:94
  220.4 3.0 all-gather.12.cloned.1.call-done
  223.4 4.9 %fusion.38 = (f32[768]{0:T(1024)S(1)}, f32[768,1024]{1,0:T(8,128)S(1)}) fusion(f32[768,1024]{1,0:T(8,128)} %copy-done.2, bf16[768,1024]{0,1:T(8,128)(2,1)} %bitcast.49, bf16[1024,1024]{0,1:T(8,128)(2,1)} %all-gather.12.cloned.1.call-done), kind=kOutput, calls=%fused_computation.73 | convolution fusion | flops 1612184832 | bytes 9964544 | tf_op jit(solution)/shard_map/dot_general | solution.py:108
  228.8 45.8 %all-gather.14.cloned.1.call-done = bf16[1024,2048]{1,0:T(8,128)(2,1)} async-done(((bf16[64,2048]{1,0:T(8,128)(2,1)}), bf16[1024,2048]{1,0:T(8,128)(2,1)}) %all-gather.14.cloned.1.call-update) | async-done | bytes 4194320 | tf_op jit(solution)/shard_map/all_gather | solution.py:114
  274.6 5.3 %fusion.22 = f32[768,2048]{1,0:T(8,128)S(1)} fusion(bf16[1024,2048]{1,0:T(8,128)(2,1)} %all-gather.14.cloned.1.call-done, f32[768,1024]{1,0:T(8,128)S(1)} %get-tuple-element.22, f32[768]{0:T(1024)S(1)} %add_rsqrt_fusion.1, f32[768]{0:T(1024)S(1)} %broadcast_multiply_fusion.1), kind=kOutput, calls=%fused_computation.41 | convolution fusion | flops 3223584768 | bytes 13637632 | tf_op jit(solution)/shard_map/dot_general | solution.py:29
  281.9 3.4 collective-permute-start
  285.3 1.5 collective-permute-start.1
  286.9 29.7 %all-gather.16.cloned.1.call-done = bf16[1024,1024]{1,0:T(8,128)(2,1)} async-done(((bf16[64,1024]{1,0:T(8,128)(2,1)}), bf16[1024,1024]{1,0:T(8,128)(2,1)}) %all-gather.16.cloned.1.call-update) | async-done | bytes 2097168 | tf_op jit(solution)/shard_map/all_gather | solution.py:127
  316.6 9.5 %fusion.39 = (f32[768]{0:T(1024)S(1)}, f32[768,1024]{1,0:T(8,128)S(1)}) fusion(f32[768,1024]{1,0:T(8,128)S(1)} %get-tuple-element.22, bf16[1024,1024]{1,0:T(8,128)(2,1)} %all-gather.16.cloned.1.call-done, bf16[768,1024]{1,0:T(8,128)(2,1)} %copy-done.4, bf16[2,1024]{1,0:T(2,128)(2,1)S(1)} %collective-permute-done.1, ...), kind=kOutput, calls=%fused_computation.74 | convolution fusion | flops 1636564224 | bytes 9993216 | tf_op jit(solution)/shard_map/dot_general | solution.py:29
  328.1 43.8 %all-gather.18.cloned.1.call-done = bf16[1536,1024]{1,0:T(8,128)(2,1)} async-done(((bf16[768,1024]{1,0:T(8,128)(2,1)}), bf16[1536,1024]{1,0:T(8,128)(2,1)}) %all-gather.18.cloned.1.call-update) | async-done | bytes 3145744 | tf_op jit(solution)/shard_map/all_gather | solution.py:132
  371.9 7.8 %fusion.5 = bf16[1,1,1536,1024]{3,2,1,0:T(8,128)(2,1)} fusion(bf16[1536,1024]{1,0:T(8,128)(2,1)} %all-gather.18.cloned.1.call-done, bf16[1,1024,1024]{2,1,0:T(8,128)(2,1)} %param.21), kind=kOutput, calls=%fused_computation.12 | convolution fusion | flops 3222798336 | bytes 8388608 | tf_op jit(solution)/shard_map/dot_general | solution.py:131
  (49 shorter events, 10.0 us)
Async XLA Ops:
  6.5 13.5 %copy-start = (bf16[1,1024,1024]{2,1,0:T(8,128)(2,1)S(1)}, bf16[1,1024,1024]{2,1,0:T(8,128)(2,1)}, u32[]{:S(2)}) copy-start(bf16[1,1024,1024]{2,1,0:T(8,128)(2,1)} %param.14) | copy-start | bytes 6291460
  6.5 72.5 %all-gather.10.cloned.1.call-start = ((), (), s32[]{:S(2)}) async-start(), calls=%async_computation.1 | async-start | bytes 6684672 | tf_op jit(solution)/shard_map/all_gather | solution.py:77
  17.2 116.3 %all-gather.20.cloned.1.call-start = ((), (), s32[]{:S(2)}) async-start(), calls=%async_computation.6 | async-start | bytes 4718592 | tf_op jit(solution)/shard_map/all_gather | solution.py:82
  63.3 24.0 %copy-start.2 = (f32[768,1024]{1,0:T(8,128)}, f32[768,1024]{1,0:T(8,128)S(1)}, u32[]{:S(2)}) copy-start(f32[768,1024]{1,0:T(8,128)S(1)} %get-tuple-element.6) | copy-start | bytes 9437188
  89.6 0.8 copy-start.5
  89.6 7.3 %copy-start.3 = (bf16[1,768,1024]{2,1,0:T(8,128)(2,1)S(1)}, bf16[1,768,1024]{2,1,0:T(8,128)(2,1)}, u32[]{:S(2)}) copy-start(bf16[1,768,1024]{2,1,0:T(8,128)(2,1)} %get-tuple-element.9) | copy-start | bytes 4718596
  89.7 99.8 %all-gather.22.cloned.1.call-start = ((), (), s32[]{:S(2)}) async-start(), calls=%async_computation.7 | async-start | bytes 4718592 | tf_op jit(solution)/shard_map/all_gather | solution.py:83
  90.4 133.0 %all-gather.12.cloned.1.call-start = ((), (), s32[]{:S(2)}) async-start(), calls=%async_computation.2 | async-start | bytes 2228224 | tf_op jit(solution)/shard_map/all_gather | solution.py:110
  95.5 179.1 %all-gather.14.cloned.1.call-start = ((), (), s32[]{:S(2)}) async-start(), calls=%async_computation.3 | async-start | bytes 4456448 | tf_op jit(solution)/shard_map/all_gather | solution.py:114
  96.1 220.5 %all-gather.16.cloned.1.call-start = ((), (), s32[]{:S(2)}) async-start(), calls=%async_computation.4 | async-start | bytes 2228224 | tf_op jit(solution)/shard_map/all_gather | solution.py:127
  96.7 275.2 %all-gather.18.cloned.1.call-start = ((), (), s32[]{:S(2)}) async-start(), calls=%async_computation.5 | async-start | bytes 4718592 | tf_op jit(solution)/shard_map/all_gather | solution.py:132
  279.9 6.9 %copy-start.6 = (bf16[5,1024]{1,0:T(8,128)(2,1)S(1)}, bf16[5,1024]{1,0:T(8,128)(2,1)}, u32[]{:S(2)}) copy-start(bf16[5,1024]{1,0:T(8,128)(2,1)} %param.19) | copy-start | bytes 30724
  280.8 1.1 copy-start.4
  281.9 34.7 %collective-permute-start = (bf16[2,1024]{1,0:T(2,128)(2,1)S(1)}, bf16[2,1024]{1,0:T(2,128)(2,1)S(1)}, u32[]{:S(2)}, u32[]{:S(2)}) collective-permute-start(bf16[2,1024]{1,0:T(2,128)(2,1)S(1)} %get-tuple-element.10), channel_id=1, source_target_pairs={{0,1},{2,3},{4,5},{6,7},{8,9},{10,11},{12,13},{14,15},{16,17},{18,... | collective-permute-start | bytes 12296 | tf_op jit(solution)/shard_map/ppermute | solution.py:16
  285.3 31.3 %collective-permute-start.1 = (bf16[2,1024]{1,0:T(2,128)(2,1)S(1)}, bf16[2,1024]{1,0:T(2,128)(2,1)S(1)}, u32[]{:S(2)}, u32[]{:S(2)}) collective-permute-start(bf16[2,1024]{1,0:T(2,128)(2,1)S(1)} %get-tuple-element.11), channel_id=1, source_target_pairs={{1,0},{3,2},{5,4},{7,6},{9,8},{11,10},{13,12},{15,14},{17,16},{19,... | collective-permute-start | bytes 12296 | tf_op jit(solution)/shard_map/ppermute | solution.py:17
  371.9 7.8 %copy-start.1 = (bf16[1,1024,1024]{2,1,0:T(8,128)(2,1)S(1)}, bf16[1,1024,1024]{2,1,0:T(8,128)(2,1)}, u32[]{:S(2)}) copy-start(bf16[1,1024,1024]{2,1,0:T(8,128)(2,1)} %param.14) | copy-start | bytes 6291460
Sparse Core Ops, SparseCore 0:
  17.3 61.7 all-gather.9
  89.8 43.5 all-gather.19
  135.0 44.8 all-gather.21
  181.9 41.4 all-gather.11
  225.4 49.1 all-gather.13
  276.6 39.9 all-gather.15
  328.2 43.6 all-gather.17
where the time goes:
time: 387 us
  waiting for transfers between devices  174 us (45%)
  matrix products  96.5 us (25%)
  blocking collectives  54 us (14%)
  other arithmetic  30.7 us (8%)
  between operations  14.4 us (4%)
  local copies, waits for them, and re-layouts  11.4 us (3%)
  starting transfers between devices  5.31 us (1%)
    all_gather x1, waiting for transfers between devices, body(): lax.all_gather(w_expand, 'dp', axis=0, tiled=True)  45.8 us
    all_gather x1, waiting for transfers between devices, body(): lax.all_gather(final_norm, 'level', axis=0, tiled=True)  43.8 us
    all_to_all x1, blocking collectives, body(): lax.all_to_all(level_terms, 'level', split_axis=0, concat_axis=0, tiled=T...  38.4 us
    all_gather x1, waiting for transfers between devices, body(): key_piece = lax.all_gather(projected[1], 'level', axis=0, tiled=True)  34.9 us
    all_gather x1, waiting for transfers between devices, body(): lax.all_gather(w_project, 'dp', axis=0, tiled=True)  29.7 us
    dot_general x1, matrix products, body(): jnp.einsum('qhd,khd->hqk', queries, key_three, preferred_element_type=jnp...  28.8 us
    dot_general x1, matrix products, body(): jnp.einsum('hqk,khd->qhd', weights.astype(jnp.bfloat16), value_three, pre...  27.7 us
    reduce_sum x1, other arithmetic, body(): weight_sum = jnp.sum(weights, axis=-1)  24.1 us
  transfers between devices with their start and end apart: 9, of which 6 were waited for; matrix products, arithmetic and copies ran while one was open for 28% of the time, Pallas kernels for 0%

commit v1 on v0

v1 whole, which is shorter than its diff:
```python
import functools
import math

import jax
import jax.numpy as jnp
from jax import lax
from jax.experimental import pallas as pl
from jax.experimental.pallas import tpu as pltpu
from jax.sharding import PartitionSpec as P

HEADS = 16
CORES = 2
LANES = 128
MESH = pl.DeviceIdType.MESH


def layer_norm(values):
    centered = values - jnp.mean(values, axis=-1, keepdims=True)
    variance = jnp.mean(centered * centered, axis=-1, keepdims=True)
    return centered * lax.rsqrt(variance + 1e-05)


def dot_f32(left, right):
    return jnp.dot(left, right, preferred_element_type=jnp.float32)


def dot_nt(left, right):
    return lax.dot_general(left, right, (((1,), (1,)), ((), ())), preferred_element_type=jnp.float32)


def chip_at(position, chips):
    position = lax.rem(position + 2 * chips, chips)
    turned = position // (chips // 2)
    return (1 - turned) * 2 * position + turned * (2 * (chips - 1 - position) + 1)


def position_of(chip, chips):
    odd = lax.rem(chip, 2)
    return (1 - odd) * (chip // 2) + odd * (chips - 1 - chip // 2)


class Ring:
    def __init__(self, full, rows, chips, sems):
        self.full, self.rows, self.chips, self.half = full, rows, chips, chips // 2
        self.send, self.recv, self.sib_send, self.sib_recv = sems
        self.device = lax.axis_index("dp")
        self.core = lax.rem(self.device, CORES)
        self.position = position_of(self.device // CORES, chips)
        self.sent = []

    def block(self, position, core, part):
        row = (chip_at(position, self.chips) * CORES + core) * self.rows
        count = self.rows
        if part is not None:
            count = self.rows // 2
            row = row + part * count
        return self.full.at[:, pl.ds(pl.multiple_of(row, count), count), :]

    def part(self, way, step):
        return way if step == self.half - 1 else None

    def origin(self, way, step):
        return self.position - (1 + step) if way == 0 else self.position + (1 + step)

    def hop(self, way, step):
        towards = self.position + 1 if way == 0 else self.position - 1
        source = self.position - step if way == 0 else self.position + step
        ref = self.block(source, self.core, self.part(way, step))
        target = chip_at(towards, self.chips) * CORES + self.core
        return pltpu.make_async_remote_copy(
            src_ref=ref,
            dst_ref=ref,
            send_sem=self.send.at[way, step],
            recv_sem=self.recv.at[way, step],
            device_id={"dp": target},
            device_id_type=MESH,
        )

    def arrival(self, way, step):
        ref = self.block(self.origin(way, step), self.core, self.part(way, step))
        return pltpu.make_async_remote_copy(
            src_ref=ref,
            dst_ref=ref,
            send_sem=self.send.at[way, step],
            recv_sem=self.recv.at[way, step],
            device_id={"dp": self.device},
            device_id_type=MESH,
        )

    def share(self, way, step, core):
        position = self.position if step < 0 else self.origin(way, step)
        ref = self.block(position, core, None if step < 0 else self.part(way, step))
        sibling = self.device + 1 - 2 * self.core
        return pltpu.make_async_remote_copy(
            src_ref=ref,
            dst_ref=ref,
            send_sem=self.sib_send.at[way, step + 1],
            recv_sem=self.sib_recv.at[way, step + 1],
            device_id={"dp": sibling},
            device_id_type=MESH,
        )

    def start(self):
        for way in range(2):
            self.hop(way, 0).start()
        self.share(0, -1, self.core).start()

    def advance(self, step):
        for way in range(2):
            self.arrival(way, step).wait_recv()
            if step + 1 < self.half:
                self.hop(way, step + 1).start()
            self.share(way, step, self.core).start()

    def finish(self):
        for way in range(2):
            for step in range(self.half):
                self.hop(way, step).wait_send()
                self.share(way, step, self.core).wait_send()
                self.share(way, step, 1 - self.core).wait_recv()
        self.share(0, -1, self.core).wait_send()
        self.share(0, -1, 1 - self.core).wait_recv()


def front_kernel(
    levels, devices, frames, width,
    meta_ref, table_ref, qkv_ref, out_ref, expand_ref, project_ref,
    attended_ref, own_ref, rest_ref,
    metas, tables, proj, embedded, normed, keys, values, queries,
    local_sem, level_send, level_recv, table_send, table_recv,
    ring_a, ring_a_recv, sib_a, sib_a_recv, ring_b, ring_b_recv, sib_b, sib_b_recv,
):
    level = lax.axis_index("level")
    device = lax.axis_index("dp")
    core = lax.rem(device, CORES)
    sibling = device + 1 - 2 * core
    chips = devices // CORES
    rows = width // devices
    columns = width // levels
    local_rows = frames // levels
    codes = table_ref.shape[0]
    half_table = codes // CORES
    position = position_of(device // CORES, chips)

    barrier = pltpu.get_barrier_semaphore()
    for shift in range(1, levels):
        pl.semaphore_signal(barrier, inc=1, device_id={"level": lax.rem(level + shift, levels)}, device_id_type=MESH)
    for other in (
        sibling,
        chip_at(position + 1, chips) * CORES + core,
        chip_at(position - 1, chips) * CORES + core,
    ):
        pl.semaphore_signal(barrier, inc=1, device_id={"dp": other}, device_id_type=MESH)
    pl.semaphore_wait(barrier, levels + 2)

    own_rows = pl.ds(pl.multiple_of(device * rows, rows), rows)
    own_columns = pl.ds(pl.multiple_of(level * columns, columns), columns)
    places = (
        (qkv_ref, proj.at[:, own_rows, own_columns]),
        (out_ref, rest_ref.at[pl.ds(0, 1), own_rows, own_columns]),
        (meta_ref, metas.at[level]),
    )
    half_rows = pl.ds(pl.multiple_of(core * half_table, half_table), half_table)
    other_half = pl.ds(pl.multiple_of((1 - core) * half_table, half_table), half_table)

    def over_level(kind, shift):
        source, place = places[kind]
        return pltpu.make_async_remote_copy(
            src_ref=source, dst_ref=place,
            send_sem=level_send.at[kind, shift], recv_sem=level_recv.at[kind, shift],
            device_id={"level": lax.rem(level + shift, levels)}, device_id_type=MESH,
        )

    def from_level(kind, shift):
        sender = lax.rem(level + levels - shift, levels)
        sender_columns = pl.ds(pl.multiple_of(sender * columns, columns), columns)
        source = places[kind][0]
        place = (
            proj.at[:, own_rows, sender_columns],
            rest_ref.at[pl.ds(0, 1), own_rows, sender_columns],
            metas.at[sender],
        )[kind]
        return pltpu.make_async_remote_copy(
            src_ref=source, dst_ref=place,
            send_sem=level_send.at[kind, shift], recv_sem=level_recv.at[kind, shift],
            device_id={"level": sender}, device_id_type=MESH,
        )

    def table_out(shift):
        return pltpu.make_async_remote_copy(
            src_ref=table_ref.at[half_rows], dst_ref=tables.at[level, half_rows],
            send_sem=table_send.at[0, shift], recv_sem=table_recv.at[0, shift],
            device_id={"level": lax.rem(level + shift, levels)}, device_id_type=MESH,
        )

    def table_at(shift, span, kind):
        sender = lax.rem(level + levels - shift, levels)
        place = tables.at[sender, span]
        return pltpu.make_async_remote_copy(
            src_ref=place, dst_ref=place,
            send_sem=table_send.at[kind, shift], recv_sem=table_recv.at[kind, shift],
            device_id={"dp": sibling}, device_id_type=MESH,
        )

    locals_ = [
        pltpu.make_async_copy(source, place, local_sem.at[i]) for i, (source, place) in enumerate(places)
    ] + [
        pltpu.make_async_copy(table_ref, tables.at[level], local_sem.at[3]),
        pltpu.make_async_copy(expand_ref.at[:, pl.ds(0, width)], rest_ref.at[1, own_rows, :], local_sem.at[4]),
        pltpu.make_async_copy(expand_ref.at[:, pl.ds(width, width)], rest_ref.at[2, own_rows, :], local_sem.at[5]),
        pltpu.make_async_copy(project_ref, rest_ref.at[3, own_rows, :], local_sem.at[6]),
    ]
    for kind in (0, 2):
        for shift in range(1, levels):
            over_level(kind, shift).start()
    for copy in locals_:
        copy.start()
    for shift in range(1, levels):
        table_out(shift).start()
    for shift in range(1, levels):
        over_level(1, shift).start()

    first = Ring(proj, rows, chips, (ring_a, ring_a_recv, sib_a, sib_a_recv))
    second = Ring(rest_ref, rows, chips, (ring_b, ring_b_recv, sib_b, sib_b_recv))

    for copy in locals_:
        copy.wait()
    for shift in range(1, levels):
        from_level(0, shift).wait_recv()
    first.start()
    for step in range(chips // 2 - 1):
        first.advance(step)
    for shift in range(1, levels):
        from_level(2, shift).wait_recv()
        table_at(shift, half_rows, 0).wait_recv()
        table_at(shift, half_rows, 1).start()
    for shift in range(1, levels):
        table_at(shift, half_rows, 1).wait_send()
        table_at(shift, other_half, 1).wait_recv()
        from_level(1, shift).wait_recv()
    first.advance(chips // 2 - 1)
    second.start()

    tile = 2 * LANES
    @pl.loop(0, frames // tile)
    def _(step):
        span = pl.ds(pl.multiple_of(step * tile, tile), tile)
        total = jnp.zeros((tile, width), jnp.float32)
        lane = lax.broadcasted_iota(jnp.int32, (tile, LANES), 1).astype(jnp.float32)
        for row in range(levels):
            ids = jnp.concatenate(
                [
                    jnp.broadcast_to(
                        metas[row, 0:1, pl.ds(pl.multiple_of(step * tile + piece * LANES, LANES), LANES)],
                        (LANES, LANES),
                    ).T
                    for piece in range(tile // LANES)
                ],
                axis=0,
            )
            onehot = jnp.concatenate(
                [
                    jnp.where(ids == lane + float(base), 1.0, 0.0).astype(jnp.bfloat16)
                    for base in range(0, codes, LANES)
                ],
                axis=1,
            )
            picked = dot_f32(onehot, tables[row])
            fill = metas[row, 8:9, 0:width]
            total = total + jnp.where(ids[:, 0:1] < 0.0, fill, picked)
        embedded[span, :] = total
        normed[span, :] = layer_norm(total).astype(jnp.bfloat16)

    own_frames = pl.ds(pl.multiple_of(level * local_rows, local_rows), local_rows)
    own_ref[...] = embedded[own_frames, :]
    first.finish()

    @pl.loop(0, frames // tile)
    def _(step):
        span = pl.ds(pl.multiple_of(step * tile, tile), tile)
        keys[span, :] = dot_f32(normed[span, :], proj[1]).astype(jnp.bfloat16)
        values[span, :] = dot_f32(normed[span, :], proj[2]).astype(jnp.bfloat16)

    head_dim = width // HEADS
    scale = head_dim ** (-0.5)
    block = math.gcd(local_rows, tile)

    @pl.loop(0, local_rows // block)
    def _(step):
        begin = pl.multiple_of(level * local_rows + step * block, block)
        to = pl.ds(pl.multiple_of(step * block, block), block)
        found = dot_f32(normed[pl.ds(begin, block), :], proj[0]).astype(jnp.bfloat16)
        queries[to, :] = found * jnp.asarray(scale, jnp.bfloat16)

    blocks = local_rows // block
    turns = (width // LANES) * blocks
    hops = chips // 2

    @pl.loop(0, turns)
    def _(turn):
        for step in range(hops):
            @pl.when(turn == (step + 1) * turns // hops - 1)
            def _():
                second.advance(step)

        pair = turn // blocks
        to = pl.ds(pl.multiple_of(lax.rem(turn, blocks) * block, block), block)
        across = pl.ds(pl.multiple_of(pair * LANES, LANES), LANES)
        query = queries[to, across]
        key = keys[:, across]
        value = values[:, across]
        lower = lax.broadcasted_iota(jnp.int32, (block, LANES), 1) < head_dim
        lower_value = lax.broadcasted_iota(jnp.int32, (frames, LANES), 1) < head_dim
        one = jnp.ones_like(value)
        zero = jnp.zeros_like(query)
        sums = []
        for low in (True, False):
            masked = jnp.where(lower, query, zero) if low else jnp.where(lower, zero, query)
            scores = dot_nt(masked, key)
            weights = jnp.exp(scores - jnp.max(scores, axis=-1, keepdims=True)).astype(jnp.bfloat16)
            extended = jnp.where(lower_value, value, one) if low else jnp.where(lower_value, one, value)
            sums.append(dot_f32(weights, extended))
        above = jnp.where(lower, sums[0], sums[1])
        below = pltpu.roll(jnp.where(lower, sums[1], sums[0]), head_dim, 1)
        attended_ref[to, across] = (above / below).astype(jnp.bfloat16)

    second.finish()
    for shift in range(1, levels):
        table_out(shift).wait_send()
        for kind in range(3):
            over_level(kind, shift).wait_send()


def front(levels, devices, ids, fill, table, w_qkv, w_out_t, w_expand, w_project):
    frames, width = ids.shape[0], table.shape[1]
    chips = devices // CORES
    local_rows = frames // levels
    span = max(frames, width)
    meta = jnp.concatenate(
        [
            jnp.broadcast_to(jnp.pad(ids, (0, span - frames)), (8, span)),
            jnp.broadcast_to(jnp.pad(fill, (0, span - width)), (8, span)),
        ]
    )
    vmem = pl.BlockSpec(memory_space=pltpu.VMEM)
    anywhere = pl.BlockSpec(memory_space=pl.ANY)
    dma = pltpu.SemaphoreType.DMA
    half = chips // 2
    bf16, f32 = jnp.bfloat16, jnp.float32
    return pl.pallas_call(
        functools.partial(front_kernel, levels, devices, frames, width),
        out_shape=(
            jax.ShapeDtypeStruct((local_rows, width), bf16),
            jax.ShapeDtypeStruct((local_rows, width), f32),
            jax.ShapeDtypeStruct((4, width, width), bf16),
        ),
        in_specs=[anywhere] * 6,
        out_specs=(vmem, vmem, vmem),
        scratch_shapes=[
            pltpu.VMEM((levels,) + meta.shape, f32),
            pltpu.VMEM((levels,) + table.shape, bf16),
            pltpu.VMEM((3, width, width), bf16),
            pltpu.VMEM((frames, width), f32),
            pltpu.VMEM((frames, width), bf16),
            pltpu.VMEM((frames, width), bf16),
            pltpu.VMEM((frames, width), bf16),
            pltpu.VMEM((local_rows, width), bf16),
            dma((7,)),
            dma((3, levels)), dma((3, levels)), dma((2, levels)), dma((2, levels)),
        ]
        + [dma((2, half)), dma((2, half)), dma((2, half + 1)), dma((2, half + 1))] * 2,
        compiler_params=pltpu.CompilerParams(
            collective_id=0, has_side_effects=True, vmem_limit_bytes=64000 * 1024
        ),
    )(meta, table, w_qkv, w_out_t, w_expand, w_project)


def with_halo(x, sides, width):
    for axis, dim in sides:
        devices, length = (lax.axis_size(axis), x.shape[dim])
        up = [(i, (i + 1) % devices) for i in range(devices - 1)]
        down = [(j, i) for i, j in up]
        last = lax.slice_in_dim(x, length - width, length, axis=dim)
        leading = lax.slice_in_dim(x, 0, width, axis=dim)
        before = lax.ppermute(last, axis, up)
        after = lax.ppermute(leading, axis, down)
        x = jnp.concatenate([before, x, after], axis=dim)
    return x


def body(
    token_ids,
    decoded_mask,
    levels_done,
    code_tables,
    mask_vectors,
    w_qkv,
    w_out,
    w_expand,
    w_depth,
    w_project,
    level_heads,
):
    frames = token_ids.shape[2]
    groups = lax.axis_size("level")
    level_index = lax.axis_index("level")
    local_rows = frames // groups
    done_count = levels_done[0]
    use_token = (level_index < done_count) | ((level_index == done_count) & (decoded_mask[0, 0] == 1))
    ids = jnp.where(use_token, token_ids[0, 0], -1).astype(jnp.float32)
    attended, own_rows, rest = front(
        groups, lax.axis_size("dp"), ids, mask_vectors[0].astype(jnp.float32), code_tables[0],
        w_qkv, w_out.T[None], w_expand, w_project,
    )
    after_attn = own_rows + dot_nt(attended, rest[0])
    normed_two = layer_norm(after_attn).astype(jnp.bfloat16)
    gated = (
        dot_f32(normed_two, rest[1]) * jax.nn.sigmoid(dot_f32(normed_two, rest[2]))
    ).astype(jnp.bfloat16)
    half_width = w_depth.shape[0] // 2
    padded = with_halo(gated, (("level", 0),), half_width)
    conv = jnp.zeros(gated.shape, jnp.float32)
    for tap_index in range(w_depth.shape[0]):
        conv = conv + padded[tap_index : tap_index + local_rows].astype(jnp.float32) * w_depth[
            tap_index
        ].astype(jnp.float32)
    activated = (conv * jax.nn.sigmoid(conv)).astype(jnp.bfloat16)
    after_conv = after_attn + dot_f32(activated, rest[3])
    final_norm = layer_norm(after_conv).astype(jnp.bfloat16)
    own_head = level_heads[0]
    logits = jnp.zeros((frames, own_head.shape[1]), jnp.bfloat16)
    pieces = [final_norm]
    for shift in range(1, groups):
        pieces.append(
            lax.ppermute(final_norm, "level", [(i, (i + shift) % groups) for i in range(groups)])
        )
    for shift, piece in enumerate(pieces):
        origin = (level_index + groups - shift) % groups
        logits = lax.dynamic_update_slice_in_dim(
            logits, dot_f32(piece, own_head).astype(jnp.bfloat16), origin * local_rows, axis=0
        )
    return logits[None, None]


def solution(mesh):
    return jax.shard_map(
        body,
        mesh=mesh,
        in_specs=(
            P("dp", "level", None),
            P("dp", "level", None),
            P("dp"),
            P("level", None, None),
            P("level", None),
            P(None, "dp", "level"),
            P("level", "dp"),
            P("dp", None),
            P(),
            P("dp", None),
            P("level", None, None),
        ),
        out_specs=P("dp", "level", None, None),
        check_vma=False,
    )
```

time: 387 us -> 178 us (0.46)
  waiting for transfers between devices: 174 us -> 35.7 us
  Pallas kernels: 0 us -> 113 us
  matrix products: 96.5 us -> 17.4 us
  blocking collectives: 54 us -> 0 us
  other arithmetic: 30.7 us -> 3.4 us
  between operations: 14.4 us -> 0.9 us
  local copies, waits for them, and re-layouts: 11.4 us -> 1.62 us
    all_gather x7 -> x0, waiting for transfers between devices: 172 us -> none  [the longest x1 45.8 us: body(): lax.all_gather(w_expand, 'dp', axis=0, tiled=True)]
    pallas_call x0 -> x1, Pallas kernels: none -> 113 us  [front(): pl.pallas_call(functools.partial(front_kernel, levels, devices, frames, w...]
    dot_general x8 -> x6, matrix products: 96.5 us -> 17.4 us  [the longest x5 12.4 us: dot_f32(): return jnp.dot(left, right, preferred_element_type=jnp.float32)]
    all_to_all x1 -> x0, blocking collectives: 38.4 us -> none  [body(): lax.all_to_all(level_terms, 'level', split_axis=0, concat_axis=0, tiled=T...]
    ppermute x0 -> x1, waiting for transfers between devices: none -> 31.7 us  [body(): lax.ppermute(final_norm, 'level', [(i, (i + shift) % groups) for i in ran...]
    reduce_sum x2 -> x0, other arithmetic: 24.7 us -> none  [the longest x1 24.1 us: body(): weight_sum = jnp.sum(weights, axis=-1)]
    all_gather x2 -> x0, blocking collectives: 15.6 us -> none  [the longest x1 10.6 us: body(): full_columns = lax.all_gather(w_qkv, 'level', axis=2, tiled=True)]
    all_gather x2 -> x0, local copies, waits for them, and re-layouts: 6.37 us -> none  [the longest x1 3.19 us: body(): value_piece = lax.all_gather(projected[2], 'level', axis=0, tiled=True)]
  transfers between devices with their start and end apart: 9 -> 3, of which waited for: 6 -> 2; matrix products, arithmetic and copies ran while one was open for 28% -> 1% of each run, Pallas kernels for 0% -> 0%
where the time goes in v1:
time: 178 us
  Pallas kernels  113 us (63%)
  waiting for transfers between devices  35.7 us (20%)
  matrix products  17.4 us (10%)
  starting transfers between devices  5.37 us (3%)
  other arithmetic  3.4 us (2%)
    pallas_call x1, Pallas kernels, front(): pl.pallas_call(functools.partial(front_kernel, levels, devices, frames, w...  113 us
    ppermute x1, waiting for transfers between devices, body(): lax.ppermute(final_norm, 'level', [(i, (i + shift) % groups) for i in ran...  31.7 us
    dot_general x5, matrix products, dot_f32(): return jnp.dot(left, right, preferred_element_type=jnp.float32)  12.4 us
    dot_general x1, matrix products, dot_nt(): lax.dot_general(left, right, (((1,), (1,)), ((), ())), preferred_element_...  5.05 us
    ppermute x1, waiting for transfers between devices, with_halo(): after = lax.ppermute(leading, axis, down)  3.97 us
    ppermute x1, starting transfers between devices, with_halo(): before = lax.ppermute(last, axis, up)  3.82 us
  transfers between devices with their start and end apart: 3, of which 2 were waited for; matrix products, arithmetic and copies ran while one was open for 1% of the time, Pallas kernels for 0%

profile of v1, /device:TPU:0, one launch (start us, length us, event | category | flops | bytes accessed | tf_op | source)
XLA Modules:
  0.0 177.8 jit_solution(3845950656424723698)
XLA Ops:
  0.7 0.7 reduce.1
  1.4 0.7 convert_reduce_fusion
  2.1 0.6 pad_maximum_fusion.2.meta_ref
  2.8 113.3 %shard_map.109 = (bf16[768,1024]{1,0:T(8,128)(2,1)}, f32[768,1024]{1,0:T(8,128)}, bf16[4,1024,1024]{2,1,0:T(8,128)(2,1)}) custom-call(f32[16,1536]{1,0:T(8,128)} %pad_maximum_fusion.2.meta_ref, bf16[1024,1024]{1,0:T(8,128)(2,1)} %bitcast.54, bf16[3,64,512]{2,1,0:T(8,128)(2,1)} %qkv_ref.1, bf16[1,64,512]{2,1,0:T(8,128)(2,1)} %bitcast.55, ...), custom_call_target="tpu_custom_call" | custom-call | tf_op jit(solution)/shard_map/pallas_call | solution.py:350
  116.1 0.0 slice-start
  116.2 5.0 %fusion.45 = (f32[768]{0:T(1024)S(1)}, f32[768,1024]{1,0:T(8,128)S(1)}) fusion(f32[768,1024]{1,0:T(8,128)} %get-tuple-element.8, bf16[768,1024]{1,0:T(8,128)(2,1)} %get-tuple-element.9, bf16[4,1024,1024]{2,1,0:T(8,128)(2,1)} %get-tuple-element.10), kind=kOutput, calls=%fused_computation.58 | convolution fusion | flops 1612184832 | bytes 9964544 | tf_op jit(solution)/shard_map/dot_general | solution.py:28
  121.2 0.4 multiply_reduce_fusion.1
  121.7 1.9 %fusion.6 = f32[768,1024]{1,0:T(8,128)S(1)} fusion(bf16[4,1024,1024]{2,1,0:T(8,128)(2,1)S(1)} %bitcast.62, f32[768,1024]{1,0:T(8,128)S(1)} %get-tuple-element.19, f32[768]{0:T(1024)S(1)} %add_rsqrt_fusion.1, f32[768]{0:T(1024)S(1)} %broadcast_multiply_fusion.1), kind=kOutput, calls=%fused_computation.12 | convolution fusion | flops 1612972032 | bytes 8396800 | tf_op jit(solution)/shard_map/dot_general | solution.py:24
  123.6 0.0 copy-start.1
  123.6 2.1 %multiply_convert_fusion.2 = bf16[768,1024]{1,0:T(8,128)(2,1)S(1)} fusion(f32[768,1024]{1,0:T(8,128)S(1)} %fusion.6, bf16[4,1024,1024]{2,1,0:T(8,128)(2,1)S(1)} %bitcast.62, f32[768,1024]{1,0:T(8,128)S(1)} %get-tuple-element.19, f32[768]{0:T(1024)S(1)} %add_rsqrt_fusion.1, f32[768]{0:T(1024)S(1)} %broadcast_multiply_fusion.1), kind=kOutput, calls=%fused_computation.3 | convolution fusion | flops 1616904192 | bytes 9969664 | tf_op jit(solution)/shard_map/dot_general | solution.py:24
  125.7 3.8 %collective-permute-start = (bf16[2,1024]{1,0:T(2,128)(2,1)S(1)}, bf16[2,1024]{1,0:T(2,128)(2,1)S(1)}, u32[]{:S(2)}, u32[]{:S(2)}) collective-permute-start(bf16[2,1024]{1,0:T(2,128)(2,1)S(1)} %get-tuple-element.11), channel_id=1, source_target_pairs={{0,1},{2,3},{4,5},{6,7},{8,9},{10,11},{12,13},{14,15},{16,17},{18,... | collective-permute-start | bytes 12296 | tf_op jit(solution)/shard_map/ppermute | solution.py:385
  129.6 1.5 collective-permute-start.1
  131.1 4.0 %collective-permute-done.1 = bf16[2,1024]{1,0:T(2,128)(2,1)S(1)} collective-permute-done((bf16[2,1024]{1,0:T(2,128)(2,1)S(1)}, bf16[2,1024]{1,0:T(2,128)(2,1)S(1)}, u32[]{:S(2)}, u32[]{:S(2)}) %collective-permute-start.1) | collective-permute-done | bytes 4128 | tf_op jit(solution)/shard_map/ppermute | solution.py:386
  135.1 3.6 %fusion.46 = (f32[768]{0:T(1024)S(1)}, f32[768,1024]{1,0:T(8,128)S(1)}) fusion(f32[768,1024]{1,0:T(8,128)S(1)} %get-tuple-element.19, bf16[4,1024,1024]{2,1,0:T(8,128)(2,1)S(1)} %bitcast.62, bf16[768,1024]{1,0:T(8,128)(2,1)S(1)} %multiply_convert_fusion.2, bf16[2,1024]{1,0:T(2,128)(2,1)S(1)} %collective-permute-done.1, ...), kind=kOutput, calls=%fused_computation.59 | convolution fusion | flops 1636564224 | bytes 9993216 | tf_op jit(solution)/shard_map/dot_general | solution.py:24
  138.7 0.4 multiply_reduce_fusion
  139.2 0.4 multiply_convert_fusion
  139.5 0.1 collective-permute-start.2
  139.6 0.0 copy-start.2
  139.6 0.4 broadcast_in_dim.30
  140.0 1.2 copy-done.2
  141.2 1.8 %bitcast_dynamic-update-slice_fusion.1 = bf16[1,1,1536,1024]{3,2,1,0:T(8,128)(2,1)S(1)} fusion(bf16[1,1,1536,1024]{3,2,1,0:T(8,128)(2,1)S(1)} %broadcast_in_dim.30, s32[]{:T(128)S(6)} %select_n.27, bf16[768,1024]{1,0:T(8,128)(2,1)S(1)} %multiply_convert_fusion, bf16[1,1024,1024]{2,1,0:T(8,128)(2,1)S(1)} %copy-done.2), kind=kOutput, calls=%fused_computation.35 | convolution fusion | flops 1611399168 | bytes 5242884 | tf_op jit(solution)/shard_map/dot_general | solution.py:24
  143.0 0.0 copy-start
  143.1 31.7 %collective-permute-done.2 = bf16[768,1024]{1,0:T(8,128)(2,1)S(1)} collective-permute-done((bf16[768,1024]{1,0:T(8,128)(2,1)S(1)}, bf16[768,1024]{1,0:T(8,128)(2,1)S(1)}, u32[]{:S(2)}, u32[]{:S(2)}) %collective-permute-start.2) | collective-permute-done | bytes 1572896 | tf_op jit(solution)/shard_map/ppermute | solution.py:435
  174.8 3.0 %bitcast_dynamic-update-slice_fusion = bf16[1,1,1536,1024]{3,2,1,0:T(8,128)(2,1)} fusion(bf16[1,1,1536,1024]{3,2,1,0:T(8,128)(2,1)} %copy-done, s32[]{:T(128)S(6)} %select_n.29, bf16[768,1024]{1,0:T(8,128)(2,1)S(1)} %collective-permute-done.2, bf16[1,1024,1024]{2,1,0:T(8,128)(2,1)S(1)} %copy-done.2), kind=kOutput, calls=%fused_computation.34 | convolution fusion | flops 1611399168 | bytes 5242884 | tf_op jit(solution)/shard_map/dot_general | solution.py:24
  (16 shorter events, 0.1 us)
Async XLA Ops:
  116.1 5.5 %slice-start = ((s8[8388608]{0:T(1024)(128)(4,1)}), s8[4194304]{0:T(1024)(128)(4,1)S(1)}, s32[]{:S(2)}) async-start(s8[8388608]{0:T(1024)(128)(4,1)} %bitcast.61), calls=%async_computation | async-start | bytes 8388608
  116.1 5.5 %slice-start.1 = ((s8[8388608]{0:T(1024)(128)(4,1)}), s8[4194304]{0:T(1024)(128)(4,1)S(1)}, s32[]{:S(2)}) async-start(s8[8388608]{0:T(1024)(128)(4,1)} %bitcast.61), calls=%async_computation.1 | async-start | bytes 8388608
  123.6 7.5 %copy-start.1 = (bf16[5,1024]{1,0:T(8,128)(2,1)S(1)}, bf16[5,1024]{1,0:T(8,128)(2,1)}, u32[]{:S(2)}) copy-start(bf16[5,1024]{1,0:T(8,128)(2,1)} %param.19) | copy-start | bytes 30724
  125.7 5.3 %collective-permute-start = (bf16[2,1024]{1,0:T(2,128)(2,1)S(1)}, bf16[2,1024]{1,0:T(2,128)(2,1)S(1)}, u32[]{:S(2)}, u32[]{:S(2)}) collective-permute-start(bf16[2,1024]{1,0:T(2,128)(2,1)S(1)} %get-tuple-element.11), channel_id=1, source_target_pairs={{0,1},{2,3},{4,5},{6,7},{8,9},{10,11},{12,13},{14,15},{16,17},{18,... | collective-permute-start | bytes 12296 | tf_op jit(solution)/shard_map/ppermute | solution.py:385
  129.6 5.5 %collective-permute-start.1 = (bf16[2,1024]{1,0:T(2,128)(2,1)S(1)}, bf16[2,1024]{1,0:T(2,128)(2,1)S(1)}, u32[]{:S(2)}, u32[]{:S(2)}) collective-permute-start(bf16[2,1024]{1,0:T(2,128)(2,1)S(1)} %get-tuple-element.12), channel_id=1, source_target_pairs={{1,0},{3,2},{5,4},{7,6},{9,8},{11,10},{13,12},{15,14},{17,16},{19,... | collective-permute-start | bytes 12296 | tf_op jit(solution)/shard_map/ppermute | solution.py:386
  139.5 35.3 %collective-permute-start.2 = (bf16[768,1024]{1,0:T(8,128)(2,1)S(1)}, bf16[768,1024]{1,0:T(8,128)(2,1)S(1)}, u32[]{:S(2)}, u32[]{:S(2)}) collective-permute-start(bf16[768,1024]{1,0:T(8,128)(2,1)S(1)} %multiply_convert_fusion), channel_id=1, source_target_pairs={{0,1},{1,0},{2,3},{3,2},{4,5},{5,4},{6,7},{7,6},{8,9},{9,8},{10,11... | collective-permute-start | bytes 4718600 | tf_op jit(solution)/shard_map/ppermute | solution.py:435
  139.6 1.6 copy-start.2
  143.0 31.8 %copy-start = (bf16[1,1,1536,1024]{3,2,1,0:T(8,128)(2,1)}, bf16[1,1,1536,1024]{3,2,1,0:T(8,128)(2,1)S(1)}, u32[]{:S(2)}) copy-start(bf16[1,1,1536,1024]{3,2,1,0:T(8,128)(2,1)S(1)} %bitcast_dynamic-update-slice_fusion.1) | copy-start | bytes 9437188

commit v2 on v1

--- a/solution.py
+++ b/solution.py
@@ -11,6 +11,7 @@
 HEADS = 16
 CORES = 2
 LANES = 128
+HALO = 16
 MESH = pl.DeviceIdType.MESH
 
 
@@ -122,11 +123,13 @@
         self.share(0, -1, 1 - self.core).wait_recv()
 
 
-def front_kernel(
+def step_kernel(
     levels, devices, frames, width,
-    meta_ref, table_ref, qkv_ref, out_ref, expand_ref, project_ref,
-    attended_ref, own_ref, rest_ref,
-    metas, tables, proj, embedded, normed, keys, values, queries,
+    meta_ref, table_ref, qkv_ref, out_ref, expand_ref, project_ref, head_ref, depth_ref,
+    logits_ref,
+    metas, tables, proj, rest_ref, embedded, normed, keys, values, queries,
+    attended, gated, final, head,
+    halo_send, halo_recv, final_send, final_recv,
     local_sem, level_send, level_recv, table_send, table_recv,
     ring_a, ring_a_recv, sib_a, sib_a_recv, ring_b, ring_b_recv, sib_b, sib_b_recv,
 ):
@@ -210,6 +213,7 @@
         pltpu.make_async_copy(expand_ref.at[:, pl.ds(width, width)], rest_ref.at[2, own_rows, :], local_sem.at[5]),
         pltpu.make_async_copy(project_ref, rest_ref.at[3, own_rows, :], local_sem.at[6]),
     ]
+    head_copy = pltpu.make_async_copy(head_ref, head, local_sem.at[7])
     for kind in (0, 2):
         for shift in range(1, levels):
             over_level(kind, shift).start()
@@ -219,6 +223,7 @@
         table_out(shift).start()
     for shift in range(1, levels):
         over_level(1, shift).start()
+    head_copy.start()
 
     first = Ring(proj, rows, chips, (ring_a, ring_a_recv, sib_a, sib_a_recv))
     second = Ring(rest_ref, rows, chips, (ring_b, ring_b_recv, sib_b, sib_b_recv))
@@ -228,7 +233,9 @@
     for shift in range(1, levels):
         from_level(0, shift).wait_recv()
     first.start()
-    for step in range(chips // 2 - 1):
+    hops = chips // 2
+    early = max(hops - 2, 0)
+    for step in range(early):
         first.advance(step)
     for shift in range(1, levels):
         from_level(2, shift).wait_recv()
@@ -238,12 +245,17 @@
         table_at(shift, half_rows, 1).wait_send()
         table_at(shift, other_half, 1).wait_recv()
         from_level(1, shift).wait_recv()
-    first.advance(chips // 2 - 1)
-    second.start()
 
     tile = 2 * LANES
     @pl.loop(0, frames // tile)
     def _(step):
+        for hop in range(early, hops):
+            @pl.when(step == (hop - early) * (frames // tile) // 2)
+            def _():
+                first.advance(hop)
+                if hop == hops - 1:
+                    second.start()
+
         span = pl.ds(pl.multiple_of(step * tile, tile), tile)
         total = jnp.zeros((tile, width), jnp.float32)
         lane = lax.broadcasted_iota(jnp.int32, (tile, LANES), 1).astype(jnp.float32)
@@ -271,8 +283,6 @@
         embedded[span, :] = total
         normed[span, :] = layer_norm(total).astype(jnp.bfloat16)
 
-    own_frames = pl.ds(pl.multiple_of(level * local_rows, local_rows), local_rows)
-    own_ref[...] = embedded[own_frames, :]
     first.finish()
 
     @pl.loop(0, frames // tile)
@@ -293,48 +303,192 @@
         queries[to, :] = found * jnp.asarray(scale, jnp.bfloat16)
 
     blocks = local_rows // block
-    turns = (width // LANES) * blocks
-    hops = chips // 2
-
-    @pl.loop(0, turns)
-    def _(turn):
-        for step in range(hops):
-            @pl.when(turn == (step + 1) * turns // hops - 1)
-            def _():
-                second.advance(step)
-
-        pair = turn // blocks
-        to = pl.ds(pl.multiple_of(lax.rem(turn, blocks) * block, block), block)
-        across = pl.ds(pl.multiple_of(pair * LANES, LANES), LANES)
-        query = queries[to, across]
-        key = keys[:, across]
-        value = values[:, across]
-        lower = lax.broadcasted_iota(jnp.int32, (block, LANES), 1) < head_dim
-        lower_value = lax.broadcasted_iota(jnp.int32, (frames, LANES), 1) < head_dim
-        one = jnp.ones_like(value)
-        zero = jnp.zeros_like(query)
-        sums = []
-        for low in (True, False):
-            masked = jnp.where(lower, query, zero) if low else jnp.where(lower, zero, query)
-            scores = dot_nt(masked, key)
-            weights = jnp.exp(scores - jnp.max(scores, axis=-1, keepdims=True)).astype(jnp.bfloat16)
-            extended = jnp.where(lower_value, value, one) if low else jnp.where(lower_value, one, value)
-            sums.append(dot_f32(weights, extended))
-        above = jnp.where(lower, sums[0], sums[1])
-        below = pltpu.roll(jnp.where(lower, sums[1], sums[0]), head_dim, 1)
-        attended_ref[to, across] = (above / below).astype(jnp.bfloat16)
-
-    second.finish()
+    pairs = width // LANES
+    turns = pairs * min(2, blocks)
+    pad = HALO
+    taps = depth_ref.shape[0]
+    odd_level = lax.rem(level, 2)
+
+    def chunk_of(owner, order):
+        odd = lax.rem(owner, 2)
+        return odd * order + (1 - odd) * (blocks - 1 - order)
+
+    def local_span(order):
+        return pl.ds(pl.multiple_of(chunk_of(level, order) * block, block), block)
+
+    def clip_span(owner, order):
+        start = owner * local_rows + chunk_of(owner, order) * block
+        return pl.ds(pl.multiple_of(start, block), block)
+
+    def halo(way):
+        source = (pl.ds(local_rows, pad), pl.ds(pad, pad))[way]
+        place = (pl.ds(0, pad), pl.ds(pad + local_rows, pad))[way]
+        target = level + 1 if way == 0 else level - 1
+        return pltpu.make_async_remote_copy(
+            src_ref=gated.at[source], dst_ref=gated.at[place],
+            send_sem=halo_send.at[way], recv_sem=halo_recv.at[way],
+            device_id={"level": target}, device_id_type=MESH,
+        )
+
+    has = (level < levels - 1, level > 0)
+
+    def halo_start(way):
+        pl.when(has[way])(lambda: halo(way).start())
+
+    def halo_wait(way):
+        pl.when(has[1 - way])(lambda: halo(way).wait_recv())
+
+    def spread(owner, order, shift, target):
+        return pltpu.make_async_remote_copy(
+            src_ref=final.at[clip_span(owner, order)], dst_ref=final.at[clip_span(owner, order)],
+            send_sem=final_send.at[order, shift], recv_sem=final_recv.at[order, shift],
+            device_id={"level": target}, device_id_type=MESH,
+        )
+
+    @pl.when(level == 0)
+    def _():
+        gated[pl.ds(0, pad), :] = jnp.zeros((pad, width), jnp.bfloat16)
+
+    @pl.when(level == levels - 1)
+    def _():
+        gated[pl.ds(pad + local_rows, pad), :] = jnp.zeros((pad, width), jnp.bfloat16)
+
+    def attend(order):
+        to = local_span(order)
+
+        @pl.loop(0, pairs)
+        def _(pair):
+            turn = order * pairs + pair
+            for step in range(hops):
+                @pl.when(turn == (step + 1) * turns // hops - 1)
+                def _():
+                    second.advance(step)
+
+            across = pl.ds(pl.multiple_of(pair * LANES, LANES), LANES)
+            query = queries[to, across]
+            key = keys[:, across]
+            value = values[:, across]
+            lower = lax.broadcasted_iota(jnp.int32, (block, LANES), 1) < head_dim
+            lower_value = lax.broadcasted_iota(jnp.int32, (frames, LANES), 1) < head_dim
+            one = jnp.ones_like(value)
+            zero = jnp.zeros_like(query)
+            sums = []
+            for low in (True, False):
+                masked = jnp.where(lower, query, zero) if low else jnp.where(lower, zero, query)
+                scores = dot_nt(masked, key)
+                weights = jnp.exp(scores - jnp.max(scores, axis=-1, keepdims=True)).astype(jnp.bfloat16)
+                extended = jnp.where(lower_value, value, one) if low else jnp.where(lower_value, one, value)
+                sums.append(dot_f32(weights, extended))
+            above = jnp.where(lower, sums[0], sums[1])
+            below = pltpu.roll(jnp.where(lower, sums[1], sums[0]), head_dim, 1)
+            attended[to, across] = (above / below).astype(jnp.bfloat16)
+
+    def gate(order):
+        own = clip_span(level, order)
+        after_attn = embedded[own, :] + dot_nt(attended[local_span(order), :], rest_ref[0])
+        embedded[own, :] = after_attn
+        normed_two = layer_norm(after_attn).astype(jnp.bfloat16)
+        mixed = dot_f32(normed_two, rest_ref[1]) * jax.nn.sigmoid(dot_f32(normed_two, rest_ref[2]))
+        start = pl.multiple_of(pad + chunk_of(level, order) * block, pad)
+        gated[pl.ds(start, block), :] = mixed.astype(jnp.bfloat16)
+
+    def convolve(order):
+        own = clip_span(level, order)
+        start = pl.multiple_of(chunk_of(level, order) * block, block)
+        window = gated[pl.ds(start, block + 2 * pad), :].astype(jnp.float32)
+        conv = jnp.zeros((block, width), jnp.float32)
+        for tap in range(taps):
+            first_row = pad - taps // 2 + tap
+            conv = conv + window[first_row : first_row + block] * depth_ref[tap : tap + 1, :]
+        activated = (conv * jax.nn.sigmoid(conv)).astype(jnp.bfloat16)
+        after_conv = embedded[own, :] + dot_f32(activated, rest_ref[3])
+        final[own, :] = layer_norm(after_conv).astype(jnp.bfloat16)
+
+    def score(owner, order):
+        span = clip_span(owner, order)
+        logits_ref[span, :] = dot_f32(final[span, :], head[...]).astype(jnp.bfloat16)
+
+    @pl.loop(0, blocks + 2)
+    def _(stage):
+        pl.when(stage < blocks)(lambda: attend(stage))
+
+        @pl.when(stage == 1)
+        def _():
+            if turns < hops:
+                for step in range(hops):
+                    if (step + 1) * turns // hops == 0:
+                        second.advance(step)
+            second.finish()
+            head_copy.wait()
+
+        @pl.when((stage >= 1) & (stage <= blocks))
+        def _():
+            gate(stage - 1)
+
+        @pl.when((stage == 1) & (odd_level == 0))
+        def _():
+            halo_start(0)
+
+        @pl.when((stage == 1) & (odd_level == 1))
+        def _():
+            halo_start(1)
+
+        @pl.when((stage == blocks) & (odd_level == 0))
+        def _():
+            halo_start(1)
+
+        @pl.when((stage == blocks) & (odd_level == 1))
+        def _():
+            halo_start(0)
+
+        @pl.when((stage == 2) & (odd_level == 0))
+        def _():
+            halo_wait(1)
+
+        @pl.when((stage == 2) & (odd_level == 1))
+        def _():
+            halo_wait(0)
+
+        @pl.when((stage == blocks + 1) & (odd_level == 0))
+        def _():
+            halo_wait(0)
+
+        @pl.when((stage == blocks + 1) & (odd_level == 1))
+        def _():
+            halo_wait(1)
+
+        @pl.when(stage >= 2)
+        def _():
+            convolve(stage - 2)
+            for shift in range(1, levels):
+                spread(level, stage - 2, shift, lax.rem(level + shift, levels)).start()
+            score(level, stage - 2)
+
+    @pl.loop(0, blocks)
+    def _(order):
+        for shift in range(1, levels):
+            sender = lax.rem(level + levels - shift, levels)
+            spread(sender, order, shift, sender).wait_recv()
+            score(sender, order)
+
+    for way in range(2):
+        pl.when(has[way])(lambda: halo(way).wait_send())
     for shift in range(1, levels):
         table_out(shift).wait_send()
         for kind in range(3):
             over_level(kind, shift).wait_send()
 
-
-def front(levels, devices, ids, fill, table, w_qkv, w_out_t, w_expand, w_project):
+    @pl.loop(0, blocks)
+    def _(order):
+        for shift in range(1, levels):
+            spread(level, order, shift, lax.rem(level + shift, levels)).wait_send()
+
+
+def decode_step(levels, devices, ids, fill, table, w_qkv, w_out_t, w_expand, w_project, head, taps):
     frames, width = ids.shape[0], table.shape[1]
     chips = devices // CORES
     local_rows = frames // levels
+    blocks = local_rows // math.gcd(local_rows, 2 * LANES)
     span = max(frames, width)
     meta = jnp.concatenate(
         [
@@ -348,44 +502,33 @@
     half = chips // 2
     bf16, f32 = jnp.bfloat16, jnp.float32
     return pl.pallas_call(
-        functools.partial(front_kernel, levels, devices, frames, width),
-        out_shape=(
-            jax.ShapeDtypeStruct((local_rows, width), bf16),
-            jax.ShapeDtypeStruct((local_rows, width), f32),
-            jax.ShapeDtypeStruct((4, width, width), bf16),
-        ),
-        in_specs=[anywhere] * 6,
-        out_specs=(vmem, vmem, vmem),
+        functools.partial(step_kernel, levels, devices, frames, width),
+        out_shape=jax.ShapeDtypeStruct((frames, head.shape[1]), bf16),
+        in_specs=[anywhere] * 7 + [vmem],
+        out_specs=vmem,
         scratch_shapes=[
             pltpu.VMEM((levels,) + meta.shape, f32),
             pltpu.VMEM((levels,) + table.shape, bf16),
             pltpu.VMEM((3, width, width), bf16),
+            pltpu.VMEM((4, width, width), bf16),
             pltpu.VMEM((frames, width), f32),
             pltpu.VMEM((frames, width), bf16),
             pltpu.VMEM((frames, width), bf16),
             pltpu.VMEM((frames, width), bf16),
             pltpu.VMEM((local_rows, width), bf16),
-            dma((7,)),
+            pltpu.VMEM((local_rows, width), bf16),
+            pltpu.VMEM((local_rows + 2 * HALO, width), bf16),
+            pltpu.VMEM((frames, width), bf16),
+            pltpu.VMEM(head.shape, bf16),
+            dma((2,)), dma((2,)), dma((blocks, levels)), dma((blocks, levels)),
+            dma((8,)),
             dma((3, levels)), dma((3, levels)), dma((2, levels)), dma((2, levels)),
         ]
         + [dma((2, half)), dma((2, half)), dma((2, half + 1)), dma((2, half + 1))] * 2,
         compiler_params=pltpu.CompilerParams(
             collective_id=0, has_side_effects=True, vmem_limit_bytes=64000 * 1024
         ),
-    )(meta, table, w_qkv, w_out_t, w_expand, w_project)
-
-
-def with_halo(x, sides, width):
-    for axis, dim in sides:
-        devices, length = (lax.axis_size(axis), x.shape[dim])
-        up = [(i, (i + 1) % devices) for i in range(devices - 1)]
-        down = [(j, i) for i, j in up]
-        last = lax.slice_in_dim(x, length - width, length, axis=dim)
-        leading = lax.slice_in_dim(x, 0, width, axis=dim)
-        before = lax.ppermute(last, axis, up)
-        after = lax.ppermute(leading, axis, down)
-        x = jnp.concatenate([before, x, after], axis=dim)
-    return x
+    )(meta, table, w_qkv, w_out_t, w_expand, w_project, head, taps)
 
 
 def body(
@@ -401,44 +544,15 @@
     w_project,
     level_heads,
 ):
-    frames = token_ids.shape[2]
     groups = lax.axis_size("level")
     level_index = lax.axis_index("level")
-    local_rows = frames // groups
     done_count = levels_done[0]
     use_token = (level_index < done_count) | ((level_index == done_count) & (decoded_mask[0, 0] == 1))
     ids = jnp.where(use_token, token_ids[0, 0], -1).astype(jnp.float32)
-    attended, own_rows, rest = front(
+    logits = decode_step(
         groups, lax.axis_size("dp"), ids, mask_vectors[0].astype(jnp.float32), code_tables[0],
-        w_qkv, w_out.T[None], w_expand, w_project,
+        w_qkv, w_out.T[None], w_expand, w_project, level_heads[0], w_depth.astype(jnp.float32),
     )
-    after_attn = own_rows + dot_nt(attended, rest[0])
-    normed_two = layer_norm(after_attn).astype(jnp.bfloat16)
-    gated = (
-        dot_f32(normed_two, rest[1]) * jax.nn.sigmoid(dot_f32(normed_two, rest[2]))
-    ).astype(jnp.bfloat16)
-    half_width = w_depth.shape[0] // 2
-    padded = with_halo(gated, (("level", 0),), half_width)
-    conv = jnp.zeros(gated.shape, jnp.float32)
-    for tap_index in range(w_depth.shape[0]):
-        conv = conv + padded[tap_index : tap_index + local_rows].astype(jnp.float32) * w_depth[
-            tap_index
-        ].astype(jnp.float32)
-    activated = (conv * jax.nn.sigmoid(conv)).astype(jnp.bfloat16)
-    after_conv = after_attn + dot_f32(activated, rest[3])
-    final_norm = layer_norm(after_conv).astype(jnp.bfloat16)
-    own_head = level_heads[0]
-    logits = jnp.zeros((frames, own_head.shape[1]), jnp.bfloat16)
-    pieces = [final_norm]
-    for shift in range(1, groups):
-        pieces.append(
-            lax.ppermute(final_norm, "level", [(i, (i + shift) % groups) for i in range(groups)])
-        )
-    for shift, piece in enumerate(pieces):
-        origin = (level_index + groups - shift) % groups
-        logits = lax.dynamic_update_slice_in_dim(
-            logits, dot_f32(piece, own_head).astype(jnp.bfloat16), origin * local_rows, axis=0
-        )
     return logits[None, None]
 
 

time: 178 us -> 164 us (0.921)
  Pallas kernels: 113 us -> 156 us
  waiting for transfers between devices: 35.7 us -> 0 us
  matrix products: 17.4 us -> 0 us
  starting transfers between devices: 5.37 us -> 0 us
  local copies, waits for them, and re-layouts: 1.62 us -> 3.87 us
    pallas_call x1, Pallas kernels: 113 us -> 156 us  [decode_step(): pl.pallas_call(functools.partial(step_kernel, levels, devices, frames, wi...]
    ppermute x3 -> x0, waiting for transfers between devices: 35.7 us -> none  [the longest x1 31.7 us: body(): lax.ppermute(final_norm, 'level', [(i, (i + shift) % groups) for i in ran...]
    dot_general x6 -> x0, matrix products: 17.4 us -> none  [the longest x5 12.4 us: dot_f32(): return jnp.dot(left, right, preferred_element_type=jnp.float32)]
    ppermute x3 -> x0, starting transfers between devices: 5.37 us -> none  [the longest x1 3.82 us: with_halo(): before = lax.ppermute(last, axis, up)]
    unnamed x10 -> x1, local copies, waits for them, and re-layouts: 1.21 us -> 3.86 us
  transfers between devices with their start and end apart: 3 -> 0, of which waited for: 2 -> 0; matrix products, arithmetic and copies ran while one was open for 1% -> 0% of each run, Pallas kernels for 0% -> 0%
where the time goes in v2:
time: 164 us
  Pallas kernels  156 us (95%)
  local copies, waits for them, and re-layouts  3.87 us (2%)
  other arithmetic  3.43 us (2%)
    pallas_call x1, Pallas kernels, decode_step(): pl.pallas_call(functools.partial(step_kernel, levels, devices, frames, wi...  156 us
    unnamed x1, local copies, waits for them, and re-layouts  3.86 us

profile of v2, /device:TPU:0, one launch (start us, length us, event | category | flops | bytes accessed | tf_op | source)
XLA Modules:
  0.0 163.8 jit_solution(2323288095238714951)
XLA Ops:
  0.7 0.7 reduce.1
  1.4 0.7 convert_reduce_fusion
  2.1 1.3 convert_element_type.14.depth_ref
  3.5 0.6 pad_maximum_fusion.meta_ref
  4.1 155.8 %shard_map.109 = bf16[1536,1024]{1,0:T(8,128)(2,1)} custom-call(f32[16,1536]{1,0:T(8,128)} %pad_maximum_fusion.meta_ref, bf16[1024,1024]{1,0:T(8,128)(2,1)} %bitcast.10, bf16[3,64,512]{2,1,0:T(8,128)(2,1)} %qkv_ref.1, bf16[1,64,512]{2,1,0:T(8,128)(2,1)} %bitcast.12, bf16[64,2048]{1,0:T(8,128)(2,1)} %expand_ref.1, bf16[64,1024]{1,0:T(8,128)(2,1)} %project_ref.1, ...), custom_call_target="tpu_custom_call" | custom-call | tf_op jit(solution)/shard_map/pallas_call | solution.py:504
  159.9 3.9 %copy.14 = bf16[1,1,1536,1024]{3,2,1,0:T(8,128)(2,1)} copy(bf16[1,1,1536,1024]{3,2,1,0:T(8,128)(2,1)} %bitcast.9) | data formatting | bytes 6291456
  (3 shorter events, 0.0 us)

commit v3 on v2

--- a/solution.py
+++ b/solution.py
@@ -225,18 +225,29 @@
         over_level(1, shift).start()
     head_copy.start()
 
-    first = Ring(proj, rows, chips, (ring_a, ring_a_recv, sib_a, sib_a_recv))
-    second = Ring(rest_ref, rows, chips, (ring_b, ring_b_recv, sib_b, sib_b_recv))
+    def rings(full, count, sems):
+        return [
+            Ring(full.at[pl.ds(piece, 1)], rows, chips, tuple(sem.at[piece] for sem in sems))
+            for piece in range(count)
+        ]
+
+    first = rings(proj, 3, (ring_a, ring_a_recv, sib_a, sib_a_recv))
+    second = rings(rest_ref, 4, (ring_b, ring_b_recv, sib_b, sib_b_recv))
 
     for copy in locals_:
         copy.wait()
     for shift in range(1, levels):
         from_level(0, shift).wait_recv()
-    first.start()
     hops = chips // 2
-    early = max(hops - 2, 0)
-    for step in range(early):
-        first.advance(step)
+    for ring in first:
+        ring.start()
+    for step in range(hops - 1):
+        for ring in first:
+            ring.advance(step)
+    for shift in range(1, levels):
+        from_level(1, shift).wait_recv()
+    for ring in second:
+        ring.start()
     for shift in range(1, levels):
         from_level(2, shift).wait_recv()
         table_at(shift, half_rows, 0).wait_recv()
@@ -244,17 +255,14 @@
     for shift in range(1, levels):
         table_at(shift, half_rows, 1).wait_send()
         table_at(shift, other_half, 1).wait_recv()
-        from_level(1, shift).wait_recv()
 
     tile = 2 * LANES
     @pl.loop(0, frames // tile)
     def _(step):
-        for hop in range(early, hops):
-            @pl.when(step == (hop - early) * (frames // tile) // 2)
+        for piece, ring in enumerate(first):
+            @pl.when(step == min(2 + piece, frames // tile - 1))
             def _():
-                first.advance(hop)
-                if hop == hops - 1:
-                    second.start()
+                ring.advance(hops - 1)
 
         span = pl.ds(pl.multiple_of(step * tile, tile), tile)
         total = jnp.zeros((tile, width), jnp.float32)
@@ -283,10 +291,16 @@
         embedded[span, :] = total
         normed[span, :] = layer_norm(total).astype(jnp.bfloat16)
 
-    first.finish()
+    for ring in first:
+        ring.finish()
 
     @pl.loop(0, frames // tile)
     def _(step):
+        for piece, ring in enumerate(second):
+            @pl.when(step == min(2 + piece, frames // tile - 1))
+            def _():
+                ring.advance(0)
+
         span = pl.ds(pl.multiple_of(step * tile, tile), tile)
         keys[span, :] = dot_f32(normed[span, :], proj[1]).astype(jnp.bfloat16)
         values[span, :] = dot_f32(normed[span, :], proj[2]).astype(jnp.bfloat16)
@@ -305,6 +319,7 @@
     blocks = local_rows // block
     pairs = width // LANES
     turns = pairs * min(2, blocks)
+    events = [(step, ring) for step in range(1, hops) for ring in second]
     pad = HALO
     taps = depth_ref.shape[0]
     odd_level = lax.rem(level, 2)
@@ -359,10 +374,10 @@
         @pl.loop(0, pairs)
         def _(pair):
             turn = order * pairs + pair
-            for step in range(hops):
-                @pl.when(turn == (step + 1) * turns // hops - 1)
+            for event, (step, ring) in enumerate(events):
+                @pl.when(turn == event * turns // len(events))
                 def _():
-                    second.advance(step)
+                    ring.advance(step)
 
             across = pl.ds(pl.multiple_of(pair * LANES, LANES), LANES)
             query = queries[to, across]
@@ -408,61 +423,46 @@
         span = clip_span(owner, order)
         logits_ref[span, :] = dot_f32(final[span, :], head[...]).astype(jnp.bfloat16)
 
-    @pl.loop(0, blocks + 2)
+    def send_and_score(order):
+        convolve(order)
+        for shift in range(1, levels):
+            spread(level, order, shift, lax.rem(level + shift, levels)).start()
+        score(level, order)
+
+    def by_parity(act, even_way):
+        pl.when(odd_level == 0)(lambda: act(even_way))
+        pl.when(odd_level == 1)(lambda: act(1 - even_way))
+
+    @pl.loop(0, blocks)
     def _(stage):
-        pl.when(stage < blocks)(lambda: attend(stage))
+        attend(stage)
 
         @pl.when(stage == 1)
         def _():
-            if turns < hops:
-                for step in range(hops):
-                    if (step + 1) * turns // hops == 0:
-                        second.advance(step)
-            second.finish()
+            for ring in second:
+                ring.finish()
             head_copy.wait()
-
-        @pl.when((stage >= 1) & (stage <= blocks))
+            gate(0)
+            by_parity(halo_start, 0)
+
+        @pl.when(stage >= 1)
         def _():
-            gate(stage - 1)
-
-        @pl.when((stage == 1) & (odd_level == 0))
+            gate(stage)
+
+        @pl.when(stage == blocks - 1)
         def _():
-            halo_start(0)
-
-        @pl.when((stage == 1) & (odd_level == 1))
+            by_parity(halo_start, 1)
+
+        @pl.when(stage == 1)
         def _():
-            halo_start(1)
-
-        @pl.when((stage == blocks) & (odd_level == 0))
+            by_parity(halo_wait, 1)
+
+        @pl.when(stage >= 1)
         def _():
-            halo_start(1)
-
-        @pl.when((stage == blocks) & (odd_level == 1))
-        def _():
-            halo_start(0)
-
-        @pl.when((stage == 2) & (odd_level == 0))
-        def _():
-            halo_wait(1)
-
-        @pl.when((stage == 2) & (odd_level == 1))
-        def _():
-            halo_wait(0)
-
-        @pl.when((stage == blocks + 1) & (odd_level == 0))
-        def _():
-            halo_wait(0)
-
-        @pl.when((stage == blocks + 1) & (odd_level == 1))
-        def _():
-            halo_wait(1)
-
-        @pl.when(stage >= 2)
-        def _():
-            convolve(stage - 2)
-            for shift in range(1, levels):
-                spread(level, stage - 2, shift, lax.rem(level + shift, levels)).start()
-            score(level, stage - 2)
+            send_and_score(stage - 1)
+
+    by_parity(halo_wait, 0)
+    send_and_score(blocks - 1)
 
     @pl.loop(0, blocks)
     def _(order):
@@ -524,7 +524,9 @@
             dma((8,)),
             dma((3, levels)), dma((3, levels)), dma((2, levels)), dma((2, levels)),
         ]
-        + [dma((2, half)), dma((2, half)), dma((2, half + 1)), dma((2, half + 1))] * 2,
+        + [
+            dma((count, 2, half + extra)) for count in (3, 4) for extra in (0, 0, 1, 1)
+        ],
         compiler_params=pltpu.CompilerParams(
             collective_id=0, has_side_effects=True, vmem_limit_bytes=64000 * 1024
         ),

time: 164 us -> 155 us (0.945)
  Pallas kernels: 156 us -> 147 us
    pallas_call x1, Pallas kernels: 156 us -> 147 us  [decode_step(): pl.pallas_call(functools.partial(step_kernel, levels, devices, frames, wi...]
where the time goes in v3:
time: 155 us
  Pallas kernels  147 us (95%)
  local copies, waits for them, and re-layouts  3.87 us (2%)
  other arithmetic  3.43 us (2%)
    pallas_call x1, Pallas kernels, decode_step(): pl.pallas_call(functools.partial(step_kernel, levels, devices, frames, wi...  147 us
    unnamed x1, local copies, waits for them, and re-layouts  3.86 us

profile of v3, /device:TPU:0, one launch (start us, length us, event | category | flops | bytes accessed | tf_op | source)
XLA Modules:
  0.0 154.6 jit_solution(2064952931749076688)
XLA Ops:
  0.7 0.7 reduce.1
  1.4 0.7 convert_reduce_fusion
  2.1 1.3 convert_element_type.14.depth_ref
  3.5 0.6 pad_maximum_fusion.meta_ref
  4.1 146.6 %shard_map.109 = bf16[1536,1024]{1,0:T(8,128)(2,1)} custom-call(f32[16,1536]{1,0:T(8,128)} %pad_maximum_fusion.meta_ref, bf16[1024,1024]{1,0:T(8,128)(2,1)} %bitcast.10, bf16[3,64,512]{2,1,0:T(8,128)(2,1)} %qkv_ref.1, bf16[1,64,512]{2,1,0:T(8,128)(2,1)} %bitcast.12, bf16[64,2048]{1,0:T(8,128)(2,1)} %expand_ref.1, bf16[64,1024]{1,0:T(8,128)(2,1)} %project_ref.1, ...), custom_call_target="tpu_custom_call" | custom-call | tf_op jit(solution)/shard_map/pallas_call | solution.py:504
  150.7 3.9 %copy.14 = bf16[1,1,1536,1024]{3,2,1,0:T(8,128)(2,1)} copy(bf16[1,1,1536,1024]{3,2,1,0:T(8,128)(2,1)} %bitcast.9) | data formatting | bytes 6291456
  (3 shorter events, 0.0 us)
